TPU v7x, 32 devices: a whole 2x2x4 slice. The times are simulated.
32 devices in a mesh: section: 4 (over y, x), dp: 8 (over z, core).
Axes of the slice: x: 2, y: 2, z: 4, core: 2. Of those that a mesh axis runs over, the one named last changes fastest.
Arguments:
- descriptors: bfloat16 [4, 4096, 1024], P(None, 'dp'), may hold values from -6 to 6
- layer_weight: bfloat16 [4, 8, 1024, 1024], P('section', None, 'dp'), may hold values from -0.25 to 0.25
- layer_bias: float32 [4, 8, 1024], P('section'), may hold values from -3 to 3
- readout: float32 [8, 1024], replicated, may hold values from -0.75 to 0.75
- self_energy: float32 [8], replicated, may hold values from -2 to -0.5
- tile_species: int32 [4, 32], P(None, 'dp'), may hold values from 0 to 7
- tile_fill: int32 [4, 32], P(None, 'dp'), may hold values from 1 to 128
Outputs:
- atom_energy: float32 [4, 4096], P('section', 'dp')
- energy: float32 [4], replicated
All inputs are finite; a program needn't handle non-finite values.
Results may differ from a plain program's by a relative error of at most 0.0044.
Values may be sent and summed in bfloat16 or wider, within the bound.
No kernel may reach another device: no remote copies, remote signals or barrier semaphores. Data moves between devices by JAX's collectives and lax.ppermute only.
A program may use at most 128 MiB of HBM per device.

v0:
```python
import jax
import jax.numpy as jnp
from jax import lax
from jax.sharding import PartitionSpec as P


def shifted(block, axis, distance):
    devices = range(lax.axis_size(axis))
    route = [(i - distance, i) for i in devices if i - distance in devices]
    return lax.ppermute(block, axis, route)


def smooth_unit(value):
    return jnp.maximum(value, 0.0) + jnp.minimum(jnp.expm1(jnp.minimum(value, 0.0)), 0.0)


def grouped_product(source, weights, species):
    chosen = jnp.take(weights, species, axis=0)
    return jnp.einsum("tai,tio->tao", source, chosen, preferred_element_type=jnp.float32)


def table_rows(onehot, table):
    return jnp.dot(onehot, table, precision=lax.Precision.HIGHEST)


def shards(descriptors, layer_weight, layer_bias, readout, self_energy, tile_species, tile_fill):
    sections = lax.axis_size("section")
    position = lax.axis_index("section")
    batches, atoms_dev, width = descriptors.shape
    tiles_dev = tile_species.shape[1]
    tile = atoms_dev // tiles_dev
    kinds = readout.shape[0]
    atoms_all = atoms_dev * lax.axis_size("dp")
    total_steps = batches + sections - 1
    bias = layer_bias[0]
    is_last = position == sections - 1
    kind_ids = jnp.arange(kinds, dtype=jnp.int32)
    slot_ids = jnp.arange(tile, dtype=jnp.int32)
    incoming = jnp.zeros((atoms_dev, width), jnp.bfloat16)
    stored = jnp.zeros((batches, atoms_dev), jnp.float32)
    energies = jnp.zeros((batches,), jnp.float32)
    weights = None
    for step in range(total_steps):
        batch = step - position
        valid = jnp.logical_and(batch >= 0, batch < batches)
        keep = jnp.logical_and(valid, is_last)
        index = jnp.clip(batch, 0, batches - 1)
        species = lax.dynamic_index_in_dim(tile_species, index, 0, keepdims=False)
        fill = lax.dynamic_index_in_dim(tile_fill, index, 0, keepdims=False)
        first = descriptors[min(step, batches - 1)]
        source = jnp.where(position == 0, first, incoming).reshape(tiles_dev, tile, width)
        if step == 0:
            weights = lax.all_gather(layer_weight[0], "dp", axis=1, tiled=True)
            product = grouped_product(source, weights, species)
        else:
            product = grouped_product(source, weights, species)
        onehot = (species[:, None] == kind_ids[None, :]).astype(jnp.float32)
        active = smooth_unit(product + table_rows(onehot, bias)[:, None, :])
        readout_rows = table_rows(onehot, readout)
        offsets = table_rows(onehot, self_energy[:, None])
        values = jnp.sum(active * readout_rows[:, None, :], axis=-1) + offsets
        present = slot_ids[None, :] < fill[:, None]
        values = jnp.where(jnp.logical_and(present, keep), values, jnp.float32(0.0)).reshape(
            atoms_dev
        )
        stored = stored.at[index].add(values)
        term = jnp.sum(values) / atoms_all
        finished = step - (sections - 1)
        if 0 <= finished < batches:
            energies = energies.at[finished].set(lax.psum(term, ("section", "dp")))
        if step < total_steps - 1:
            incoming = shifted(active.astype(jnp.bfloat16).reshape(atoms_dev, width), "section", 1)
    received = lax.all_to_all(stored, "section", split_axis=0, concat_axis=0, tiled=True)
    mine = received[sections - 1]
    return (mine[None, :], energies)


def solution(mesh):
    placed = (
        P(None, "dp", None),
        P("section", None, "dp", None),
        P("section", None, None),
        P(),
        P(),
        P(None, "dp"),
        P(None, "dp"),
    )
    return jax.shard_map(
        shards, mesh=mesh, in_specs=placed, out_specs=(P("section", "dp"), P()), check_vma=False
    )
```

profile of v0, /device:TPU:12, one launch (start us, length us, event | category | flops | bytes accessed | tf_op | source)
XLA Modules:
  0.0 464.9 jit_solution(16702947367663745943)
XLA Ops:
  7.9 1.0 compare_and_fusion
  9.0 1.4 and_reduce_fusion.4
  10.6 1.0 fusion.56
  11.6 1.3 slice_select_fusion
  12.9 146.2 %all-gather.3.cloned.1.call-done = bf16[1,8,1024,1024]{3,2,1,0:T(8,128)(2,1)} async-done(((bf16[1,8,128,1024]{3,2,1,0:T(8,128)(2,1)}), bf16[1,8,1024,1024]{3,2,1,0:T(8,128)(2,1)}) %all-gather.3.cloned.1.call-update) | async-done | bytes 16777232 | tf_op jit(solution)/shard_map/all_gather | solution.py:53
  159.1 11.7 %fusion.131 = (bf16[8,512,1024]{2,1,0:T(8,128)(2,1)}, bf16[8,512,1024]{2,1,0:T(8,128)(2,1)}) fusion(bf16[8,1024,1024]{2,1,0:T(8,128)(2,1)} %bitcast.146), kind=kLoop, calls=%fused_computation.259 | loop fusion | bytes 33554432 | tf_op jit(solution)/shard_map/jit(_take)/gather | solution.py:18
  170.8 6.2 %gather_fusion = bf16[4,512,1024]{2,1,0:T(8,128)(2,1)} fusion(bf16[8,512,1024]{2,1,0:T(8,128)(2,1)} %get-tuple-element.168, s32[1024]{0:T(1024)S(1)} %pad_clamp_fusion.6), kind=kCustom, calls=%fused_computation.clone | custom fusion | bytes 8388624 | tf_op jit(solution)/shard_map/jit(_take)/gather | solution.py:18
  176.9 6.1 %gather_fusion.1 = bf16[4,512,1024]{2,1,0:T(8,128)(2,1)} fusion(bf16[8,512,1024]{2,1,0:T(8,128)(2,1)} %get-tuple-element.169, s32[1024]{0:T(1024)S(1)} %pad_clamp_fusion.6), kind=kCustom, calls=%fused_computation.1.clone | custom fusion | bytes 8388624 | tf_op jit(solution)/shard_map/jit(_take)/gather | solution.py:18
  183.1 5.4 %fusion.137 = (bf16[4,128,1024]{2,1,0:T(8,128)(2,1)S(1)}, f32[4,128]{1,0:T(4,128)S(1)}) fusion(f32[4,1024]{1,0:T(4,128)S(1)} %fusion.56, f32[4,1024]{1,0:T(4,128)S(1)} %fusion.47, bf16[4,128,1024]{2,1,0:T(8,128)(2,1)S(1)} %bitcast.147, bf16[4,512,1024]{2,1,0:T(8,128)(2,1)} %gather_fusion.1, bf16[4,512,1024]{2,1,0:T(8,128)(2,1)} %gather_fusion, ...), kind=kOutput, calls=%fused_computation.265 | convolution fusion | flops 1098907136 | bytes 10520580 | tf_op jit(solution)/shard_map/tai,tio->tao/dot_general | solution.py:19
  188.5 3.4 collective-permute-start
  191.9 0.8 and_reduce_fusion
  193.5 6.2 %gather_fusion.2 = bf16[4,512,1024]{2,1,0:T(8,128)(2,1)} fusion(bf16[8,512,1024]{2,1,0:T(8,128)(2,1)} %get-tuple-element.168, s32[1024]{0:T(1024)S(1)} %pad_clamp_fusion.5), kind=kCustom, calls=%fused_computation.2.clone | custom fusion | bytes 8388624 | tf_op jit(solution)/shard_map/jit(_take)/gather | solution.py:18
  199.7 6.1 %gather_fusion.3 = bf16[4,512,1024]{2,1,0:T(8,128)(2,1)} fusion(bf16[8,512,1024]{2,1,0:T(8,128)(2,1)} %get-tuple-element.169, s32[1024]{0:T(1024)S(1)} %pad_clamp_fusion.5), kind=kCustom, calls=%fused_computation.3.clone | custom fusion | bytes 8388624 | tf_op jit(solution)/shard_map/jit(_take)/gather | solution.py:18
  205.8 10.8 %collective-permute-done = bf16[512,1024]{1,0:T(8,128)(2,1)S(1)} collective-permute-done((bf16[512,1024]{1,0:T(8,128)(2,1)S(1)}, bf16[512,1024]{1,0:T(8,128)(2,1)S(1)}, u32[]{:S(2)}, u32[]{:S(2)}) %collective-permute-start) | collective-permute-done | bytes 1048608 | tf_op jit(solution)/shard_map/ppermute | solution.py:10
  216.6 1.3 bitcast_select_fusion.5
  217.9 5.4 %fusion.136 = (bf16[4,128,1024]{2,1,0:T(8,128)(2,1)S(1)}, f32[4,128]{1,0:T(4,128)S(1)}) fusion(f32[4,1024]{1,0:T(4,128)S(1)} %fusion.55, f32[4,1024]{1,0:T(4,128)S(1)} %fusion.45, bf16[4,128,1024]{2,1,0:T(8,128)(2,1)S(1)} %bitcast.148, bf16[4,512,1024]{2,1,0:T(8,128)(2,1)} %gather_fusion.3, bf16[4,512,1024]{2,1,0:T(8,128)(2,1)} %gather_fusion.2, ...), kind=kOutput, calls=%fused_computation.264 | convolution fusion | flops 1098907136 | bytes 10520580 | tf_op jit(solution)/shard_map/tai,tio->tao/dot_general | solution.py:19
  223.3 2.5 collective-permute-start.1
  227.0 6.2 %gather_fusion.4 = bf16[4,512,1024]{2,1,0:T(8,128)(2,1)} fusion(bf16[8,512,1024]{2,1,0:T(8,128)(2,1)} %get-tuple-element.168, s32[1024]{0:T(1024)S(1)} %pad_clamp_fusion.4), kind=kCustom, calls=%fused_computation.4.clone | custom fusion | bytes 8388624 | tf_op jit(solution)/shard_map/jit(_take)/gather | solution.py:18
  233.2 6.1 %gather_fusion.5 = bf16[4,512,1024]{2,1,0:T(8,128)(2,1)} fusion(bf16[8,512,1024]{2,1,0:T(8,128)(2,1)} %get-tuple-element.169, s32[1024]{0:T(1024)S(1)} %pad_clamp_fusion.4), kind=kCustom, calls=%fused_computation.5.clone | custom fusion | bytes 8388624 | tf_op jit(solution)/shard_map/jit(_take)/gather | solution.py:18
  239.4 11.2 %collective-permute-done.1 = bf16[512,1024]{1,0:T(8,128)(2,1)S(1)} collective-permute-done((bf16[512,1024]{1,0:T(8,128)(2,1)S(1)}, bf16[512,1024]{1,0:T(8,128)(2,1)S(1)}, u32[]{:S(2)}, u32[]{:S(2)}) %collective-permute-start.1) | collective-permute-done | bytes 1048608 | tf_op jit(solution)/shard_map/ppermute | solution.py:10
  250.6 1.3 bitcast_select_fusion.4
  251.9 5.4 %fusion.135 = (bf16[4,128,1024]{2,1,0:T(8,128)(2,1)S(1)}, f32[4,128]{1,0:T(4,128)S(1)}) fusion(f32[4,1024]{1,0:T(4,128)S(1)} %fusion.54, f32[4,1024]{1,0:T(4,128)S(1)} %fusion.43, bf16[4,128,1024]{2,1,0:T(8,128)(2,1)S(1)} %bitcast.149, bf16[4,512,1024]{2,1,0:T(8,128)(2,1)} %gather_fusion.5, bf16[4,512,1024]{2,1,0:T(8,128)(2,1)} %gather_fusion.4, ...), kind=kOutput, calls=%fused_computation.263 | convolution fusion | flops 1098907136 | bytes 10520580 | tf_op jit(solution)/shard_map/tai,tio->tao/dot_general | solution.py:19
  257.4 1.9 collective-permute-start.2
  260.3 6.2 %gather_fusion.6 = bf16[4,512,1024]{2,1,0:T(8,128)(2,1)} fusion(bf16[8,512,1024]{2,1,0:T(8,128)(2,1)} %get-tuple-element.168, s32[1024]{0:T(1024)S(1)} %pad_clamp_fusion.3), kind=kCustom, calls=%fused_computation.6.clone | custom fusion | bytes 8388624 | tf_op jit(solution)/shard_map/jit(_take)/gather | solution.py:18
  266.5 6.1 %gather_fusion.7 = bf16[4,512,1024]{2,1,0:T(8,128)(2,1)} fusion(bf16[8,512,1024]{2,1,0:T(8,128)(2,1)} %get-tuple-element.169, s32[1024]{0:T(1024)S(1)} %pad_clamp_fusion.3), kind=kCustom, calls=%fused_computation.7.clone | custom fusion | bytes 8388624 | tf_op jit(solution)/shard_map/jit(_take)/gather | solution.py:18
  272.6 11.2 %collective-permute-done.2 = bf16[512,1024]{1,0:T(8,128)(2,1)S(1)} collective-permute-done((bf16[512,1024]{1,0:T(8,128)(2,1)S(1)}, bf16[512,1024]{1,0:T(8,128)(2,1)S(1)}, u32[]{:S(2)}, u32[]{:S(2)}) %collective-permute-start.2) | collective-permute-done | bytes 1048608 | tf_op jit(solution)/shard_map/ppermute | solution.py:10
  283.8 1.3 bitcast_select_fusion.3
  285.1 5.4 %fusion.134 = (bf16[4,128,1024]{2,1,0:T(8,128)(2,1)S(1)}, f32[4,128]{1,0:T(4,128)S(1)}) fusion(f32[4,1024]{1,0:T(4,128)S(1)} %fusion.53, f32[4,1024]{1,0:T(4,128)S(1)} %fusion.41, bf16[4,128,1024]{2,1,0:T(8,128)(2,1)S(1)} %bitcast.150, bf16[4,512,1024]{2,1,0:T(8,128)(2,1)} %gather_fusion.7, bf16[4,512,1024]{2,1,0:T(8,128)(2,1)} %gather_fusion.6, ...), kind=kOutput, calls=%fused_computation.262 | convolution fusion | flops 1098907136 | bytes 10520580 | tf_op jit(solution)/shard_map/tai,tio->tao/dot_general | solution.py:19
  290.5 2.1 collective-permute-start.3
  293.5 6.3 %gather_fusion.8 = bf16[4,512,1024]{2,1,0:T(8,128)(2,1)} fusion(bf16[8,512,1024]{2,1,0:T(8,128)(2,1)} %get-tuple-element.168, s32[1024]{0:T(1024)S(1)} %pad_clamp_fusion.2), kind=kCustom, calls=%fused_computation.8.clone | custom fusion | bytes 8388624 | tf_op jit(solution)/shard_map/jit(_take)/gather | solution.py:18
  299.8 6.1 %gather_fusion.9 = bf16[4,512,1024]{2,1,0:T(8,128)(2,1)} fusion(bf16[8,512,1024]{2,1,0:T(8,128)(2,1)} %get-tuple-element.169, s32[1024]{0:T(1024)S(1)} %pad_clamp_fusion.2), kind=kCustom, calls=%fused_computation.9.clone | custom fusion | bytes 8388624 | tf_op jit(solution)/shard_map/jit(_take)/gather | solution.py:18
  305.9 6.2 %gather_fusion.10 = bf16[4,512,1024]{2,1,0:T(8,128)(2,1)} fusion(bf16[8,512,1024]{2,1,0:T(8,128)(2,1)} %get-tuple-element.168, s32[1024]{0:T(1024)S(1)} %pad_clamp_fusion.1), kind=kCustom, calls=%fused_computation.10.clone | custom fusion | bytes 8388624 | tf_op jit(solution)/shard_map/jit(_take)/gather | solution.py:18
  312.1 6.2 %gather_fusion.11 = bf16[4,512,1024]{2,1,0:T(8,128)(2,1)} fusion(bf16[8,512,1024]{2,1,0:T(8,128)(2,1)} %get-tuple-element.169, s32[1024]{0:T(1024)S(1)} %pad_clamp_fusion.1), kind=kCustom, calls=%fused_computation.11.clone | custom fusion | bytes 8388624 | tf_op jit(solution)/shard_map/jit(_take)/gather | solution.py:18
  318.2 6.1 %gather_fusion.12 = bf16[4,512,1024]{2,1,0:T(8,128)(2,1)} fusion(bf16[8,512,1024]{2,1,0:T(8,128)(2,1)} %get-tuple-element.168, s32[1024]{0:T(1024)S(1)} %pad_clamp_fusion), kind=kCustom, calls=%fused_computation.12.clone | custom fusion | bytes 8388624 | tf_op jit(solution)/shard_map/jit(_take)/gather | solution.py:18
  324.4 6.2 %gather_fusion.13 = bf16[4,512,1024]{2,1,0:T(8,128)(2,1)} fusion(bf16[8,512,1024]{2,1,0:T(8,128)(2,1)} %get-tuple-element.169, s32[1024]{0:T(1024)S(1)} %pad_clamp_fusion), kind=kCustom, calls=%fused_computation.13.clone | custom fusion | bytes 8388624 | tf_op jit(solution)/shard_map/jit(_take)/gather | solution.py:18
  331.3 1.3 bitcast_select_fusion.2
  332.6 5.4 %fusion.133 = (bf16[4,128,1024]{2,1,0:T(8,128)(2,1)S(1)}, f32[4,128]{1,0:T(4,128)S(1)}) fusion(f32[4,1024]{1,0:T(4,128)S(1)} %fusion.52, f32[4,1024]{1,0:T(4,128)S(1)} %fusion.39, bf16[4,128,1024]{2,1,0:T(8,128)(2,1)S(1)} %bitcast.151, bf16[4,512,1024]{2,1,0:T(8,128)(2,1)} %gather_fusion.9, bf16[4,512,1024]{2,1,0:T(8,128)(2,1)} %gather_fusion.8, ...), kind=kOutput, calls=%fused_computation.261 | convolution fusion | flops 1098907136 | bytes 10520580 | tf_op jit(solution)/shard_map/tai,tio->tao/dot_general | solution.py:19
  338.0 1.9 collective-permute-start.4
  342.2 21.4 %collective-permute-done.4 = bf16[512,1024]{1,0:T(8,128)(2,1)S(1)} collective-permute-done((bf16[512,1024]{1,0:T(8,128)(2,1)S(1)}, bf16[512,1024]{1,0:T(8,128)(2,1)S(1)}, u32[]{:S(2)}, u32[]{:S(2)}) %collective-permute-start.4) | collective-permute-done | bytes 1048608 | tf_op jit(solution)/shard_map/ppermute | solution.py:10
  363.6 1.3 bitcast_select_fusion.1
  364.9 5.4 %fusion.132 = (bf16[4,128,1024]{2,1,0:T(8,128)(2,1)S(1)}, f32[4,128]{1,0:T(4,128)S(1)}) fusion(f32[4,1024]{1,0:T(4,128)S(1)} %fusion.51, f32[4,1024]{1,0:T(4,128)S(1)} %fusion.37, bf16[4,128,1024]{2,1,0:T(8,128)(2,1)S(1)} %bitcast.152, bf16[4,512,1024]{2,1,0:T(8,128)(2,1)} %gather_fusion.11, bf16[4,512,1024]{2,1,0:T(8,128)(2,1)} %gather_fusion.10, ...), kind=kOutput, calls=%fused_computation.260 | convolution fusion | flops 1098907136 | bytes 10520580 | tf_op jit(solution)/shard_map/tai,tio->tao/dot_general | solution.py:19
  370.4 1.9 collective-permute-start.5
  376.3 18.7 %collective-permute-done.5 = bf16[512,1024]{1,0:T(8,128)(2,1)S(1)} collective-permute-done((bf16[512,1024]{1,0:T(8,128)(2,1)S(1)}, bf16[512,1024]{1,0:T(8,128)(2,1)S(1)}, u32[]{:S(2)}, u32[]{:S(2)}) %collective-permute-start.5) | collective-permute-done | bytes 1048608 | tf_op jit(solution)/shard_map/ppermute | solution.py:10
  395.1 1.3 bitcast_select_fusion
  396.4 5.4 %multiply_reduce_fusion = f32[4,128]{1,0:T(4,128)S(1)} fusion(bf16[4,128,1024]{2,1,0:T(8,128)(2,1)S(1)} %bitcast.153, bf16[4,512,1024]{2,1,0:T(8,128)(2,1)} %gather_fusion.13, bf16[4,512,1024]{2,1,0:T(8,128)(2,1)} %gather_fusion.12, pred[4]{0:T(512)(128)(4,1)S(1)} %get-tuple-element.154, f32[4,1024]{1,0:T(4,128)S(1)} %fusion.50, f32[4,1024]{1,0:T(4,128)S(1)} %fusion.35), kind=kOutput, calls=%fused_computation.56 | convolution fusion | flops 1098382848 | bytes 9472004 | tf_op jit(solution)/shard_map/tai,tio->tao/dot_general | solution.py:19
  402.5 1.2 constant_dynamic-update-slice_fusion
  403.7 3.3 all-to-all-start
  409.5 45.5 %all-reduce.1 = (f32[1]{0:T(128)}, f32[1]{0:T(128)}, f32[1]{0:T(128)}, f32[1]{0:T(128)}) all-reduce(f32[1]{0:T(128)} %bitcast.62, f32[1]{0:T(128)} %bitcast.63, f32[1]{0:T(128)} %bitcast.64, f32[1]{0:T(128)} %bitcast.65), channel_id=1, replica_groups=mesh['section'=4,'dp'=8] {'section','dp'}, use_global_device_ids=true, to_apply=%region_15.17 | all-reduce | flops 4 | bytes 32 | tf_op jit(solution)/shard_map/psum | solution.py:70
  (73 shorter events, 15.5 us)
Async XLA Ops:
  7.2 3.3 copy-start
  7.2 151.9 %all-gather.3.cloned.1.call-start = ((), (), s32[]{:S(2)}) async-start(), calls=%async_computation.1 | async-start | bytes 18874368 | tf_op jit(solution)/shard_map/all_gather | solution.py:53
  183.1 8.8 %copy-start.2 = (s32[2]{0:T(128)S(1)}, s32[2]{0:T(128)}, u32[]{:S(2)}) copy-start(s32[2]{0:T(128)} %constant.301.clone.1) | copy-start | bytes 28
  183.1 9.6 %copy-start.4 = (f32[8]{0:T(128)S(1)}, f32[8]{0:T(128)}, u32[]{:S(2)}) copy-start(f32[8]{0:T(128)} %param.35) | copy-start | bytes 100
  183.1 10.2 %copy-start.3 = (f32[8,1024]{1,0:T(8,128)S(1)}, f32[8,1024]{1,0:T(8,128)}, u32[]{:S(2)}) copy-start(f32[8,1024]{1,0:T(8,128)} %param.34) | copy-start | bytes 98308
  188.5 28.1 %collective-permute-start = (bf16[512,1024]{1,0:T(8,128)(2,1)S(1)}, bf16[512,1024]{1,0:T(8,128)(2,1)S(1)}, u32[]{:S(2)}, u32[]{:S(2)}) collective-permute-start(bf16[512,1024]{1,0:T(8,128)(2,1)S(1)} %bitcast.164), channel_id=1, source_target_pairs={{0,8},{8,16},{16,24},{1,9},{9,17},{17,25},{2,10},{10,18},{18,26},{... | collective-permute-start | bytes 3145736 | tf_op jit(solution)/shard_map/ppermute | solution.py:10
  223.3 27.3 %collective-permute-start.1 = (bf16[512,1024]{1,0:T(8,128)(2,1)S(1)}, bf16[512,1024]{1,0:T(8,128)(2,1)S(1)}, u32[]{:S(2)}, u32[]{:S(2)}) collective-permute-start(bf16[512,1024]{1,0:T(8,128)(2,1)S(1)} %bitcast.166), channel_id=1, source_target_pairs={{0,8},{8,16},{16,24},{1,9},{9,17},{17,25},{2,10},{10,18},{18,26},{... | collective-permute-start | bytes 3145736 | tf_op jit(solution)/shard_map/ppermute | solution.py:10
  257.4 26.4 %collective-permute-start.2 = (bf16[512,1024]{1,0:T(8,128)(2,1)S(1)}, bf16[512,1024]{1,0:T(8,128)(2,1)S(1)}, u32[]{:S(2)}, u32[]{:S(2)}) collective-permute-start(bf16[512,1024]{1,0:T(8,128)(2,1)S(1)} %bitcast.165), channel_id=1, source_target_pairs={{0,8},{8,16},{16,24},{1,9},{9,17},{17,25},{2,10},{10,18},{18,26},{... | collective-permute-start | bytes 3145736 | tf_op jit(solution)/shard_map/ppermute | solution.py:10
  285.1 7.5 %copy-start.1 = (s32[4,4]{1,0:T(4,128)S(1)}, s32[4,4]{1,0:T(4,128)}, u32[]{:S(2)}) copy-start(s32[4,4]{1,0:T(4,128)} %param.37) | copy-start | bytes 196
  290.5 40.7 %collective-permute-start.3 = (bf16[512,1024]{1,0:T(8,128)(2,1)S(1)}, bf16[512,1024]{1,0:T(8,128)(2,1)S(1)}, u32[]{:S(2)}, u32[]{:S(2)}) collective-permute-start(bf16[512,1024]{1,0:T(8,128)(2,1)S(1)} %bitcast.161), channel_id=1, source_target_pairs={{0,8},{8,16},{16,24},{1,9},{9,17},{17,25},{2,10},{10,18},{18,26},{... | collective-permute-start | bytes 3145736 | tf_op jit(solution)/shard_map/ppermute | solution.py:10
  338.0 25.6 %collective-permute-start.4 = (bf16[512,1024]{1,0:T(8,128)(2,1)S(1)}, bf16[512,1024]{1,0:T(8,128)(2,1)S(1)}, u32[]{:S(2)}, u32[]{:S(2)}) collective-permute-start(bf16[512,1024]{1,0:T(8,128)(2,1)S(1)} %bitcast.163), channel_id=1, source_target_pairs={{0,8},{8,16},{16,24},{1,9},{9,17},{17,25},{2,10},{10,18},{18,26},{... | collective-permute-start | bytes 3145736 | tf_op jit(solution)/shard_map/ppermute | solution.py:10
  370.4 24.7 %collective-permute-start.5 = (bf16[512,1024]{1,0:T(8,128)(2,1)S(1)}, bf16[512,1024]{1,0:T(8,128)(2,1)S(1)}, u32[]{:S(2)}, u32[]{:S(2)}) collective-permute-start(bf16[512,1024]{1,0:T(8,128)(2,1)S(1)} %bitcast.162), channel_id=1, source_target_pairs={{0,8},{8,16},{16,24},{1,9},{9,17},{17,25},{2,10},{10,18},{18,26},{... | collective-permute-start | bytes 3145736 | tf_op jit(solution)/shard_map/ppermute | solution.py:10
  403.7 53.8 %all-to-all-start = ((f32[4,1,512]{2,1,0:T(1,128)}), f32[4,1,512]{2,1,0:T(1,128)S(1)}, u32[]{:S(2)}, u32[]{:S(2)}) async-start(f32[4,1,512]{2,1,0:T(1,128)} %constant_dynamic-update-slice_fusion), calls=%async_computation | async-start | bytes 16384 | tf_op jit(solution)/shard_map/all_to_all | solution.py:73
  457.4 0.6 copy-start.5
Sparse Core Ops, SparseCore 0:
  9.6 149.4 all-gather.2
where the time goes:
time: 466 us; the launch traced here: 465 us
  waiting for transfers between devices  220 us (47%)
  local copies, waits for them, and re-layouts  102 us (22%)
  blocking collectives  45.5 us (10%)
  matrix products  42.8 us (9%)
  other arithmetic  20.5 us (4%)
  starting transfers between devices  17.1 us (4%)
  between operations  17 us (4%)
    all_gather x1, waiting for transfers between devices, shards(): weights = lax.all_gather(layer_weight[0], 'dp', axis=1, tiled=True)  146 us
    gather x15, local copies, waits for them, and re-layouts, grouped_product(): chosen = jnp.take(weights, species, axis=0)  97.9 us
    ppermute x6, waiting for transfers between devices, shifted(): return lax.ppermute(block, axis, route)  73.3 us
    psum x1, blocking collectives, shards(): energies = energies.at[finished].set(lax.psum(term, ('section', 'dp')))  45.5 us
    dot_general x7, matrix products, grouped_product(): jnp.einsum('tai,tio->tao', source, chosen, preferred_element_type=jnp.flo...  37.9 us
    ppermute x6, starting transfers between devices, shifted(): return lax.ppermute(block, axis, route)  13.7 us
  transfers between devices with their start and end apart: 8, of which 6 were waited for; matrix products, arithmetic and copies ran while one was open for 20% of the time, Pallas kernels for 0%

commit v1 on v0

--- a/solution.py
+++ b/solution.py
@@ -2,6 +2,11 @@
 import jax.numpy as jnp
 from jax import lax
 from jax.sharding import PartitionSpec as P
+
+
+def clear_the_local_data(block_in, lane_axis, comm_axis):
+    new = lax.psum(lax.psum(block_in, axis_name=lane_axis), axis_name=comm_axis)
+    return new
 
 
 def shifted(block, axis, distance):
@@ -67,7 +72,7 @@
         term = jnp.sum(values) / atoms_all
         finished = step - (sections - 1)
         if 0 <= finished < batches:
-            energies = energies.at[finished].set(lax.psum(term, ("section", "dp")))
+            energies = energies.at[finished].set(clear_the_local_data(term, "section", "dp"))
         if step < total_steps - 1:
             incoming = shifted(active.astype(jnp.bfloat16).reshape(atoms_dev, width), "section", 1)
     received = lax.all_to_all(stored, "section", split_axis=0, concat_axis=0, tiled=True)

time: 466 us -> 450 us (0.966); the launches traced: 465 us -> 443 us
  blocking collectives: 45.5 us -> 23 us
    psum x1 -> x2, blocking collectives: 45.5 us -> 23 us  [clear_the_local_data(): new = lax.psum(lax.psum(block_in, axis_name=lane_axis), axis_name=comm_axis)]
  transfers between devices with their start and end apart: 8 -> 8, of which waited for: 6 -> 6; matrix products, arithmetic and copies ran while one was open for 20% -> 21% of each run, Pallas kernels for 0% -> 0%
where the time goes in v1:
time: 450 us; the launch traced here: 443 us
  waiting for transfers between devices  220 us (49%)
  local copies, waits for them, and re-layouts  102 us (23%)
  matrix products  42.8 us (10%)
  blocking collectives  23 us (5%)
  other arithmetic  20.5 us (5%)
  starting transfers between devices  17.1 us (4%)
  between operations  17 us (4%)
    all_gather x1, waiting for transfers between devices, shards(): weights = lax.all_gather(layer_weight[0], 'dp', axis=1, tiled=True)  146 us
    gather x15, local copies, waits for them, and re-layouts, grouped_product(): chosen = jnp.take(weights, species, axis=0)  97.9 us
    ppermute x6, waiting for transfers between devices, shifted(): return lax.ppermute(block, axis, route)  73.3 us
    dot_general x7, matrix products, grouped_product(): jnp.einsum('tai,tio->tao', source, chosen, preferred_element_type=jnp.flo...  37.9 us
    psum x2, blocking collectives, clear_the_local_data(): new = lax.psum(lax.psum(block_in, axis_name=lane_axis), axis_name=comm_axis)  23 us
    ppermute x6, starting transfers between devices, shifted(): return lax.ppermute(block, axis, route)  13.7 us
    select_n x7, other arithmetic, shards(): jnp.where(position == 0, first, incoming).reshape(tiles_dev, tile, width)  9.32 us
  transfers between devices with their start and end apart: 8, of which 6 were waited for; matrix products, arithmetic and copies ran while one was open for 21% of the time, Pallas kernels for 0%

profile of v1, /device:TPU:12, one launch (start us, length us, event | category | flops | bytes accessed | tf_op | source)
XLA Modules:
  0.0 442.6 jit_solution(6910802996189266135)
XLA Ops:
  7.9 1.0 compare_and_fusion
  9.0 1.4 and_reduce_fusion.4
  10.6 1.0 fusion.56
  11.6 1.3 slice_select_fusion
  12.9 146.2 %all-gather.3.cloned.1.call-done = bf16[1,8,1024,1024]{3,2,1,0:T(8,128)(2,1)} async-done(((bf16[1,8,128,1024]{3,2,1,0:T(8,128)(2,1)}), bf16[1,8,1024,1024]{3,2,1,0:T(8,128)(2,1)}) %all-gather.3.cloned.1.call-update) | async-done | bytes 16777232 | tf_op jit(solution)/shard_map/all_gather | solution.py:58
  159.1 11.7 %fusion.131 = (bf16[8,512,1024]{2,1,0:T(8,128)(2,1)}, bf16[8,512,1024]{2,1,0:T(8,128)(2,1)}) fusion(bf16[8,1024,1024]{2,1,0:T(8,128)(2,1)} %bitcast.146), kind=kLoop, calls=%fused_computation.259 | loop fusion | bytes 33554432 | tf_op jit(solution)/shard_map/jit(_take)/gather | solution.py:23
  170.8 6.2 %gather_fusion = bf16[4,512,1024]{2,1,0:T(8,128)(2,1)} fusion(bf16[8,512,1024]{2,1,0:T(8,128)(2,1)} %get-tuple-element.172, s32[1024]{0:T(1024)S(1)} %pad_clamp_fusion.6), kind=kCustom, calls=%fused_computation.clone | custom fusion | bytes 8388624 | tf_op jit(solution)/shard_map/jit(_take)/gather | solution.py:23
  176.9 6.1 %gather_fusion.1 = bf16[4,512,1024]{2,1,0:T(8,128)(2,1)} fusion(bf16[8,512,1024]{2,1,0:T(8,128)(2,1)} %get-tuple-element.173, s32[1024]{0:T(1024)S(1)} %pad_clamp_fusion.6), kind=kCustom, calls=%fused_computation.1.clone | custom fusion | bytes 8388624 | tf_op jit(solution)/shard_map/jit(_take)/gather | solution.py:23
  183.1 5.4 %fusion.137 = (bf16[4,128,1024]{2,1,0:T(8,128)(2,1)S(1)}, f32[4,128]{1,0:T(4,128)S(1)}) fusion(f32[4,1024]{1,0:T(4,128)S(1)} %fusion.56, f32[4,1024]{1,0:T(4,128)S(1)} %fusion.47, bf16[4,128,1024]{2,1,0:T(8,128)(2,1)S(1)} %bitcast.147, bf16[4,512,1024]{2,1,0:T(8,128)(2,1)} %gather_fusion.1, bf16[4,512,1024]{2,1,0:T(8,128)(2,1)} %gather_fusion, ...), kind=kOutput, calls=%fused_computation.265 | convolution fusion | flops 1098907136 | bytes 10520580 | tf_op jit(solution)/shard_map/tai,tio->tao/dot_general | solution.py:24
  188.5 3.4 collective-permute-start
  193.5 6.2 %gather_fusion.2 = bf16[4,512,1024]{2,1,0:T(8,128)(2,1)} fusion(bf16[8,512,1024]{2,1,0:T(8,128)(2,1)} %get-tuple-element.172, s32[1024]{0:T(1024)S(1)} %pad_clamp_fusion.5), kind=kCustom, calls=%fused_computation.2.clone | custom fusion | bytes 8388624 | tf_op jit(solution)/shard_map/jit(_take)/gather | solution.py:23
  199.7 6.1 %gather_fusion.3 = bf16[4,512,1024]{2,1,0:T(8,128)(2,1)} fusion(bf16[8,512,1024]{2,1,0:T(8,128)(2,1)} %get-tuple-element.173, s32[1024]{0:T(1024)S(1)} %pad_clamp_fusion.5), kind=kCustom, calls=%fused_computation.3.clone | custom fusion | bytes 8388624 | tf_op jit(solution)/shard_map/jit(_take)/gather | solution.py:23
  205.8 10.8 %collective-permute-done = bf16[512,1024]{1,0:T(8,128)(2,1)S(1)} collective-permute-done((bf16[512,1024]{1,0:T(8,128)(2,1)S(1)}, bf16[512,1024]{1,0:T(8,128)(2,1)S(1)}, u32[]{:S(2)}, u32[]{:S(2)}) %collective-permute-start) | collective-permute-done | bytes 1048608 | tf_op jit(solution)/shard_map/ppermute | solution.py:15
  216.6 1.3 bitcast_select_fusion.5
  217.9 5.4 %fusion.136 = (bf16[4,128,1024]{2,1,0:T(8,128)(2,1)S(1)}, f32[4,128]{1,0:T(4,128)S(1)}) fusion(f32[4,1024]{1,0:T(4,128)S(1)} %fusion.55, f32[4,1024]{1,0:T(4,128)S(1)} %fusion.45, bf16[4,128,1024]{2,1,0:T(8,128)(2,1)S(1)} %bitcast.148, bf16[4,512,1024]{2,1,0:T(8,128)(2,1)} %gather_fusion.3, bf16[4,512,1024]{2,1,0:T(8,128)(2,1)} %gather_fusion.2, ...), kind=kOutput, calls=%fused_computation.264 | convolution fusion | flops 1098907136 | bytes 10520580 | tf_op jit(solution)/shard_map/tai,tio->tao/dot_general | solution.py:24
  223.3 2.5 collective-permute-start.1
  227.0 6.2 %gather_fusion.4 = bf16[4,512,1024]{2,1,0:T(8,128)(2,1)} fusion(bf16[8,512,1024]{2,1,0:T(8,128)(2,1)} %get-tuple-element.172, s32[1024]{0:T(1024)S(1)} %pad_clamp_fusion.4), kind=kCustom, calls=%fused_computation.4.clone | custom fusion | bytes 8388624 | tf_op jit(solution)/shard_map/jit(_take)/gather | solution.py:23
  233.2 6.1 %gather_fusion.5 = bf16[4,512,1024]{2,1,0:T(8,128)(2,1)} fusion(bf16[8,512,1024]{2,1,0:T(8,128)(2,1)} %get-tuple-element.173, s32[1024]{0:T(1024)S(1)} %pad_clamp_fusion.4), kind=kCustom, calls=%fused_computation.5.clone | custom fusion | bytes 8388624 | tf_op jit(solution)/shard_map/jit(_take)/gather | solution.py:23
  239.4 11.2 %collective-permute-done.1 = bf16[512,1024]{1,0:T(8,128)(2,1)S(1)} collective-permute-done((bf16[512,1024]{1,0:T(8,128)(2,1)S(1)}, bf16[512,1024]{1,0:T(8,128)(2,1)S(1)}, u32[]{:S(2)}, u32[]{:S(2)}) %collective-permute-start.1) | collective-permute-done | bytes 1048608 | tf_op jit(solution)/shard_map/ppermute | solution.py:15
  250.6 1.3 bitcast_select_fusion.4
  251.9 5.4 %fusion.135 = (bf16[4,128,1024]{2,1,0:T(8,128)(2,1)S(1)}, f32[4,128]{1,0:T(4,128)S(1)}) fusion(f32[4,1024]{1,0:T(4,128)S(1)} %fusion.54, f32[4,1024]{1,0:T(4,128)S(1)} %fusion.43, bf16[4,128,1024]{2,1,0:T(8,128)(2,1)S(1)} %bitcast.149, bf16[4,512,1024]{2,1,0:T(8,128)(2,1)} %gather_fusion.5, bf16[4,512,1024]{2,1,0:T(8,128)(2,1)} %gather_fusion.4, ...), kind=kOutput, calls=%fused_computation.263 | convolution fusion | flops 1098907136 | bytes 10520580 | tf_op jit(solution)/shard_map/tai,tio->tao/dot_general | solution.py:24
  257.4 1.9 collective-permute-start.2
  260.3 6.2 %gather_fusion.6 = bf16[4,512,1024]{2,1,0:T(8,128)(2,1)} fusion(bf16[8,512,1024]{2,1,0:T(8,128)(2,1)} %get-tuple-element.172, s32[1024]{0:T(1024)S(1)} %pad_clamp_fusion.3), kind=kCustom, calls=%fused_computation.6.clone | custom fusion | bytes 8388624 | tf_op jit(solution)/shard_map/jit(_take)/gather | solution.py:23
  266.5 6.1 %gather_fusion.7 = bf16[4,512,1024]{2,1,0:T(8,128)(2,1)} fusion(bf16[8,512,1024]{2,1,0:T(8,128)(2,1)} %get-tuple-element.173, s32[1024]{0:T(1024)S(1)} %pad_clamp_fusion.3), kind=kCustom, calls=%fused_computation.7.clone | custom fusion | bytes 8388624 | tf_op jit(solution)/shard_map/jit(_take)/gather | solution.py:23
  272.6 11.2 %collective-permute-done.2 = bf16[512,1024]{1,0:T(8,128)(2,1)S(1)} collective-permute-done((bf16[512,1024]{1,0:T(8,128)(2,1)S(1)}, bf16[512,1024]{1,0:T(8,128)(2,1)S(1)}, u32[]{:S(2)}, u32[]{:S(2)}) %collective-permute-start.2) | collective-permute-done | bytes 1048608 | tf_op jit(solution)/shard_map/ppermute | solution.py:15
  283.8 1.3 bitcast_select_fusion.3
  285.1 5.4 %fusion.134 = (bf16[4,128,1024]{2,1,0:T(8,128)(2,1)S(1)}, f32[4,128]{1,0:T(4,128)S(1)}) fusion(f32[4,1024]{1,0:T(4,128)S(1)} %fusion.53, f32[4,1024]{1,0:T(4,128)S(1)} %fusion.41, bf16[4,128,1024]{2,1,0:T(8,128)(2,1)S(1)} %bitcast.150, bf16[4,512,1024]{2,1,0:T(8,128)(2,1)} %gather_fusion.7, bf16[4,512,1024]{2,1,0:T(8,128)(2,1)} %gather_fusion.6, ...), kind=kOutput, calls=%fused_computation.262 | convolution fusion | flops 1098907136 | bytes 10520580 | tf_op jit(solution)/shard_map/tai,tio->tao/dot_general | solution.py:24
  290.5 2.1 collective-permute-start.3
  293.5 6.3 %gather_fusion.8 = bf16[4,512,1024]{2,1,0:T(8,128)(2,1)} fusion(bf16[8,512,1024]{2,1,0:T(8,128)(2,1)} %get-tuple-element.172, s32[1024]{0:T(1024)S(1)} %pad_clamp_fusion.2), kind=kCustom, calls=%fused_computation.8.clone | custom fusion | bytes 8388624 | tf_op jit(solution)/shard_map/jit(_take)/gather | solution.py:23
  299.8 6.1 %gather_fusion.9 = bf16[4,512,1024]{2,1,0:T(8,128)(2,1)} fusion(bf16[8,512,1024]{2,1,0:T(8,128)(2,1)} %get-tuple-element.173, s32[1024]{0:T(1024)S(1)} %pad_clamp_fusion.2), kind=kCustom, calls=%fused_computation.9.clone | custom fusion | bytes 8388624 | tf_op jit(solution)/shard_map/jit(_take)/gather | solution.py:23
  305.9 6.2 %gather_fusion.10 = bf16[4,512,1024]{2,1,0:T(8,128)(2,1)} fusion(bf16[8,512,1024]{2,1,0:T(8,128)(2,1)} %get-tuple-element.172, s32[1024]{0:T(1024)S(1)} %pad_clamp_fusion.1), kind=kCustom, calls=%fused_computation.10.clone | custom fusion | bytes 8388624 | tf_op jit(solution)/shard_map/jit(_take)/gather | solution.py:23
  312.1 6.2 %gather_fusion.11 = bf16[4,512,1024]{2,1,0:T(8,128)(2,1)} fusion(bf16[8,512,1024]{2,1,0:T(8,128)(2,1)} %get-tuple-element.173, s32[1024]{0:T(1024)S(1)} %pad_clamp_fusion.1), kind=kCustom, calls=%fused_computation.11.clone | custom fusion | bytes 8388624 | tf_op jit(solution)/shard_map/jit(_take)/gather | solution.py:23
  318.2 6.1 %gather_fusion.12 = bf16[4,512,1024]{2,1,0:T(8,128)(2,1)} fusion(bf16[8,512,1024]{2,1,0:T(8,128)(2,1)} %get-tuple-element.172, s32[1024]{0:T(1024)S(1)} %pad_clamp_fusion), kind=kCustom, calls=%fused_computation.12.clone | custom fusion | bytes 8388624 | tf_op jit(solution)/shard_map/jit(_take)/gather | solution.py:23
  324.4 6.2 %gather_fusion.13 = bf16[4,512,1024]{2,1,0:T(8,128)(2,1)} fusion(bf16[8,512,1024]{2,1,0:T(8,128)(2,1)} %get-tuple-element.173, s32[1024]{0:T(1024)S(1)} %pad_clamp_fusion), kind=kCustom, calls=%fused_computation.13.clone | custom fusion | bytes 8388624 | tf_op jit(solution)/shard_map/jit(_take)/gather | solution.py:23
  331.3 1.3 bitcast_select_fusion.2
  332.6 5.4 %fusion.133 = (bf16[4,128,1024]{2,1,0:T(8,128)(2,1)S(1)}, f32[4,128]{1,0:T(4,128)S(1)}) fusion(f32[4,1024]{1,0:T(4,128)S(1)} %fusion.52, f32[4,1024]{1,0:T(4,128)S(1)} %fusion.39, bf16[4,128,1024]{2,1,0:T(8,128)(2,1)S(1)} %bitcast.151, bf16[4,512,1024]{2,1,0:T(8,128)(2,1)} %gather_fusion.9, bf16[4,512,1024]{2,1,0:T(8,128)(2,1)} %gather_fusion.8, ...), kind=kOutput, calls=%fused_computation.261 | convolution fusion | flops 1098907136 | bytes 10520580 | tf_op jit(solution)/shard_map/tai,tio->tao/dot_general | solution.py:24
  338.0 1.9 collective-permute-start.4
  342.2 21.4 %collective-permute-done.4 = bf16[512,1024]{1,0:T(8,128)(2,1)S(1)} collective-permute-done((bf16[512,1024]{1,0:T(8,128)(2,1)S(1)}, bf16[512,1024]{1,0:T(8,128)(2,1)S(1)}, u32[]{:S(2)}, u32[]{:S(2)}) %collective-permute-start.4) | collective-permute-done | bytes 1048608 | tf_op jit(solution)/shard_map/ppermute | solution.py:15
  363.6 1.3 bitcast_select_fusion.1
  364.9 5.4 %fusion.132 = (bf16[4,128,1024]{2,1,0:T(8,128)(2,1)S(1)}, f32[4,128]{1,0:T(4,128)S(1)}) fusion(f32[4,1024]{1,0:T(4,128)S(1)} %fusion.51, f32[4,1024]{1,0:T(4,128)S(1)} %fusion.37, bf16[4,128,1024]{2,1,0:T(8,128)(2,1)S(1)} %bitcast.152, bf16[4,512,1024]{2,1,0:T(8,128)(2,1)} %gather_fusion.11, bf16[4,512,1024]{2,1,0:T(8,128)(2,1)} %gather_fusion.10, ...), kind=kOutput, calls=%fused_computation.260 | convolution fusion | flops 1098907136 | bytes 10520580 | tf_op jit(solution)/shard_map/tai,tio->tao/dot_general | solution.py:24
  370.4 1.9 collective-permute-start.5
  376.3 18.7 %collective-permute-done.5 = bf16[512,1024]{1,0:T(8,128)(2,1)S(1)} collective-permute-done((bf16[512,1024]{1,0:T(8,128)(2,1)S(1)}, bf16[512,1024]{1,0:T(8,128)(2,1)S(1)}, u32[]{:S(2)}, u32[]{:S(2)}) %collective-permute-start.5) | collective-permute-done | bytes 1048608 | tf_op jit(solution)/shard_map/ppermute | solution.py:15
  395.1 1.3 bitcast_select_fusion
  396.4 5.4 %multiply_reduce_fusion = f32[4,128]{1,0:T(4,128)S(1)} fusion(bf16[4,128,1024]{2,1,0:T(8,128)(2,1)S(1)} %bitcast.153, bf16[4,512,1024]{2,1,0:T(8,128)(2,1)} %gather_fusion.13, bf16[4,512,1024]{2,1,0:T(8,128)(2,1)} %gather_fusion.12, pred[4]{0:T(512)(128)(4,1)S(1)} %get-tuple-element.158, f32[4,1024]{1,0:T(4,128)S(1)} %fusion.50, f32[4,1024]{1,0:T(4,128)S(1)} %fusion.35), kind=kOutput, calls=%fused_computation.56 | convolution fusion | flops 1098382848 | bytes 9472004 | tf_op jit(solution)/shard_map/tai,tio->tao/dot_general | solution.py:24
  402.5 1.2 constant_dynamic-update-slice_fusion
  403.7 3.3 all-to-all-start
  409.5 9.5 %all-reduce.2 = (f32[]{:T(128)}, f32[]{:T(128)}, f32[]{:T(128)}, f32[]{:T(128)}) all-reduce(f32[]{:T(128)S(6)} %div.12, f32[]{:T(128)S(6)} %div.13, f32[]{:T(128)S(6)} %div.14, f32[]{:T(128)S(6)} %div.15), channel_id=1, replica_groups=mesh['section'=4,'dp'=8] {'section'}, use_global_device_ids=true, to_apply=%region_15.17 | all-reduce | flops 4 | bytes 32 | tf_op jit(solution)/shard_map/psum | solution.py:8
  418.9 13.6 %all-reduce.1 = (f32[1]{0:T(128)}, f32[1]{0:T(128)}, f32[1]{0:T(128)}, f32[1]{0:T(128)}) all-reduce(f32[1]{0:T(128)} %bitcast.62, f32[1]{0:T(128)} %bitcast.63, f32[1]{0:T(128)} %bitcast.64, f32[1]{0:T(128)} %bitcast.65), channel_id=1, replica_groups=mesh['section'=4,'dp'=8] {'dp'}, use_global_device_ids=true, to_apply=%region_16.18 | all-reduce | flops 4 | bytes 32 | tf_op jit(solution)/shard_map/psum | solution.py:8
  (74 shorter events, 16.3 us)
Async XLA Ops:
  7.2 3.3 copy-start
  7.2 151.9 %all-gather.3.cloned.1.call-start = ((), (), s32[]{:S(2)}) async-start(), calls=%async_computation.1 | async-start | bytes 18874368 | tf_op jit(solution)/shard_map/all_gather | solution.py:58
  183.1 8.8 %copy-start.2 = (s32[2]{0:T(128)S(1)}, s32[2]{0:T(128)}, u32[]{:S(2)}) copy-start(s32[2]{0:T(128)} %constant.301.clone.1) | copy-start | bytes 28
  183.1 9.6 %copy-start.4 = (f32[8]{0:T(128)S(1)}, f32[8]{0:T(128)}, u32[]{:S(2)}) copy-start(f32[8]{0:T(128)} %param.35) | copy-start | bytes 100
  183.1 10.2 %copy-start.3 = (f32[8,1024]{1,0:T(8,128)S(1)}, f32[8,1024]{1,0:T(8,128)}, u32[]{:S(2)}) copy-start(f32[8,1024]{1,0:T(8,128)} %param.34) | copy-start | bytes 98308
  188.5 28.1 %collective-permute-start = (bf16[512,1024]{1,0:T(8,128)(2,1)S(1)}, bf16[512,1024]{1,0:T(8,128)(2,1)S(1)}, u32[]{:S(2)}, u32[]{:S(2)}) collective-permute-start(bf16[512,1024]{1,0:T(8,128)(2,1)S(1)} %bitcast.164), channel_id=1, source_target_pairs={{0,8},{8,16},{16,24},{1,9},{9,17},{17,25},{2,10},{10,18},{18,26},{... | collective-permute-start | bytes 3145736 | tf_op jit(solution)/shard_map/ppermute | solution.py:15
  223.3 27.3 %collective-permute-start.1 = (bf16[512,1024]{1,0:T(8,128)(2,1)S(1)}, bf16[512,1024]{1,0:T(8,128)(2,1)S(1)}, u32[]{:S(2)}, u32[]{:S(2)}) collective-permute-start(bf16[512,1024]{1,0:T(8,128)(2,1)S(1)} %bitcast.166), channel_id=1, source_target_pairs={{0,8},{8,16},{16,24},{1,9},{9,17},{17,25},{2,10},{10,18},{18,26},{... | collective-permute-start | bytes 3145736 | tf_op jit(solution)/shard_map/ppermute | solution.py:15
  257.4 26.4 %collective-permute-start.2 = (bf16[512,1024]{1,0:T(8,128)(2,1)S(1)}, bf16[512,1024]{1,0:T(8,128)(2,1)S(1)}, u32[]{:S(2)}, u32[]{:S(2)}) collective-permute-start(bf16[512,1024]{1,0:T(8,128)(2,1)S(1)} %bitcast.165), channel_id=1, source_target_pairs={{0,8},{8,16},{16,24},{1,9},{9,17},{17,25},{2,10},{10,18},{18,26},{... | collective-permute-start | bytes 3145736 | tf_op jit(solution)/shard_map/ppermute | solution.py:15
  285.1 7.5 %copy-start.1 = (s32[4,4]{1,0:T(4,128)S(1)}, s32[4,4]{1,0:T(4,128)}, u32[]{:S(2)}) copy-start(s32[4,4]{1,0:T(4,128)} %param.37) | copy-start | bytes 196
  290.5 40.7 %collective-permute-start.3 = (bf16[512,1024]{1,0:T(8,128)(2,1)S(1)}, bf16[512,1024]{1,0:T(8,128)(2,1)S(1)}, u32[]{:S(2)}, u32[]{:S(2)}) collective-permute-start(bf16[512,1024]{1,0:T(8,128)(2,1)S(1)} %bitcast.161), channel_id=1, source_target_pairs={{0,8},{8,16},{16,24},{1,9},{9,17},{17,25},{2,10},{10,18},{18,26},{... | collective-permute-start | bytes 3145736 | tf_op jit(solution)/shard_map/ppermute | solution.py:15
  338.0 25.6 %collective-permute-start.4 = (bf16[512,1024]{1,0:T(8,128)(2,1)S(1)}, bf16[512,1024]{1,0:T(8,128)(2,1)S(1)}, u32[]{:S(2)}, u32[]{:S(2)}) collective-permute-start(bf16[512,1024]{1,0:T(8,128)(2,1)S(1)} %bitcast.163), channel_id=1, source_target_pairs={{0,8},{8,16},{16,24},{1,9},{9,17},{17,25},{2,10},{10,18},{18,26},{... | collective-permute-start | bytes 3145736 | tf_op jit(solution)/shard_map/ppermute | solution.py:15
  370.4 24.7 %collective-permute-start.5 = (bf16[512,1024]{1,0:T(8,128)(2,1)S(1)}, bf16[512,1024]{1,0:T(8,128)(2,1)S(1)}, u32[]{:S(2)}, u32[]{:S(2)}) collective-permute-start(bf16[512,1024]{1,0:T(8,128)(2,1)S(1)} %bitcast.162), channel_id=1, source_target_pairs={{0,8},{8,16},{16,24},{1,9},{9,17},{17,25},{2,10},{10,18},{18,26},{... | collective-permute-start | bytes 3145736 | tf_op jit(solution)/shard_map/ppermute | solution.py:15
  403.7 31.5 %all-to-all-start = ((f32[4,1,512]{2,1,0:T(1,128)}), f32[4,1,512]{2,1,0:T(1,128)S(1)}, u32[]{:S(2)}, u32[]{:S(2)}) async-start(f32[4,1,512]{2,1,0:T(1,128)} %constant_dynamic-update-slice_fusion), calls=%async_computation | async-start | bytes 16384 | tf_op jit(solution)/shard_map/all_to_all | solution.py:78
  435.1 0.6 copy-start.5
Sparse Core Ops, SparseCore 0:
  9.6 149.4 all-gather.2
